TPU v7x, 32 devices: a whole 2x2x4 slice. The times are simulated.
32 devices in a mesh: blk: 4 (over x, core), group: 8 (over z, y).
Axes of the slice: x: 2, y: 2, z: 4, core: 2. Of those that a mesh axis runs over, the one named last changes fastest.
Arguments:
- queries: bfloat16 [8, 512, 2048], P('group', 'blk'), may hold values from -300 to 300
- normed: bfloat16 [8, 512, 2048], P('group', 'blk'), may hold values from -6 to 6
- key_weight_copies: bfloat16 [8, 2048, 512], P('group', 'blk'), may hold values from -0.125 to 0.125
- value_weight_copies: bfloat16 [8, 2048, 512], P('group', 'blk'), may hold values from -0.125 to 0.125
- owner: int32 [4], replicated, may hold values from 0 to 7
Outputs:
- cache_keys: bfloat16 [8, 512, 512], P('group', 'blk')
- cache_values: bfloat16 [8, 512, 512], P('group', 'blk')
- attended: bfloat16 [8, 512, 2048], P('group', 'blk')
Inputs may be any that keep to these rules, and one draw needn't show every extreme that they name: `owner`: learner group index of each block of projection rows, below the number of actor groups.
All inputs are finite; a program needn't handle non-finite values.
Results may differ from a plain program's by a relative error of at most 0.011.
Values may be sent and summed in bfloat16 or wider, within the bound.
A program may use at most 64 MiB of HBM per device.

v0:
```python
import math

import jax
import jax.numpy as jnp
from jax import lax
from jax.sharding import PartitionSpec as P

QUERY_HEADS = 16
KEY_VALUE_HEADS = 4
HEAD_SIZE = 128


def spread(value, axis, source):
    kept = jnp.where(lax.axis_index(axis) == source, value, 0).astype(value.dtype)
    return lax.psum(kept, axis)


def rotate(unshaped_rows, positions):
    half_dim = HEAD_SIZE // 2
    inverse_freq = jnp.exp(
        jnp.arange(half_dim).astype(jnp.float32) * (-2.0 * math.log(500000.0) / HEAD_SIZE)
    )
    angles = positions.astype(jnp.float32)[:, None] * inverse_freq[None, :]
    cos_table = jnp.cos(angles)[:, None, :]
    sin_table = jnp.sin(angles)[:, None, :]
    reshaped_rows = unshaped_rows.reshape(unshaped_rows.shape[0], KEY_VALUE_HEADS, HEAD_SIZE)
    first_half = reshaped_rows[..., :half_dim]
    second_half = reshaped_rows[..., half_dim:]
    transposed_rows = jnp.concatenate(
        [
            first_half * cos_table - second_half * sin_table,
            second_half * cos_table + first_half * sin_table,
        ],
        axis=-1,
    )
    return transposed_rows.reshape(unshaped_rows.shape[0], KEY_VALUE_HEADS * HEAD_SIZE)


def body(queries, normed, key_weight_copies, value_weight_copies, owner):
    input_rows = normed[0]
    token_rows = input_rows.shape[0]
    owner_group = lax.dynamic_index_in_dim(owner, lax.axis_index("blk"), 0, keepdims=False)
    shard_keys, shard_values = (
        spread(key_weight_copies[0], "group", owner_group),
        spread(value_weight_copies[0], "group", owner_group),
    )
    pieces = (
        lax.all_gather(shard_keys, "blk", axis=0, tiled=True),
        lax.all_gather(shard_values, "blk", axis=0, tiled=True),
    )
    key_raw = jnp.dot(input_rows, pieces[0], preferred_element_type=jnp.float32)
    value_raw = jnp.dot(input_rows, pieces[1], preferred_element_type=jnp.float32)
    positions = lax.axis_index("blk") * token_rows + jnp.arange(token_rows, dtype=jnp.int32)
    cache_keys = rotate(key_raw, positions).astype(jnp.bfloat16)
    cache_values = value_raw.astype(jnp.bfloat16)
    query_head_grid = queries[0].reshape(
        token_rows, KEY_VALUE_HEADS, QUERY_HEADS // KEY_VALUE_HEADS, HEAD_SIZE
    )
    score_scale = HEAD_SIZE ** (-0.5)
    start_state = (
        jnp.full((KEY_VALUE_HEADS, QUERY_HEADS // KEY_VALUE_HEADS, token_rows), -1e30, jnp.float32),
        jnp.zeros((KEY_VALUE_HEADS, QUERY_HEADS // KEY_VALUE_HEADS, token_rows), jnp.float32),
        jnp.zeros(
            (KEY_VALUE_HEADS, QUERY_HEADS // KEY_VALUE_HEADS, token_rows, HEAD_SIZE), jnp.float32
        ),
    )
    pieces = (
        lax.all_gather(cache_keys, "blk", axis=0, tiled=True),
        lax.all_gather(cache_values, "blk", axis=0, tiled=True),
    )
    key_count = pieces[0].shape[0]
    key_row_width = math.gcd(key_count, 512)

    def one_block(block_turn, state_in):
        row_top, row_total, weighted_values = state_in
        offset = block_turn * key_row_width
        key_part = lax.dynamic_slice_in_dim(pieces[0], offset, key_row_width, 0).reshape(
            key_row_width, KEY_VALUE_HEADS, HEAD_SIZE
        )
        value_part = lax.dynamic_slice_in_dim(pieces[1], offset, key_row_width, 0).reshape(
            key_row_width, KEY_VALUE_HEADS, HEAD_SIZE
        )
        scores = (
            jnp.einsum(
                "lewc,jec->ewlj", query_head_grid, key_part, preferred_element_type=jnp.float32
            )
            * score_scale
        )
        key_pos = offset + jnp.arange(key_row_width, dtype=jnp.int32)
        allowed = key_pos[None, :] <= positions[:, None]
        scores = jnp.where(allowed, scores, -jnp.inf)
        new_top = jnp.maximum(row_top, jnp.max(scores, axis=-1))
        fade_by = jnp.exp(row_top - new_top)
        prob_block = jnp.exp(scores - new_top[..., None])
        row_total = row_total * fade_by + jnp.sum(prob_block, axis=-1)
        weighted_values = weighted_values * fade_by[..., None] + jnp.einsum(
            "lxbp,plj->lxbj",
            prob_block.astype(jnp.bfloat16),
            value_part,
            preferred_element_type=jnp.float32,
        )
        return (new_top, row_total, weighted_values)

    row_top, row_total, weighted_values = lax.fori_loop(
        0, key_count // key_row_width, one_block, start_state
    )
    attended = (
        (weighted_values / row_total[..., None])
        .transpose(2, 0, 1, 3)
        .reshape(token_rows, QUERY_HEADS * HEAD_SIZE)
        .astype(jnp.bfloat16)
    )
    return (cache_keys[None], cache_values[None], attended[None])


def solution(mesh):
    placed = (
        P("group", "blk", None),
        P("group", "blk", None),
        P("group", "blk", None),
        P("group", "blk", None),
        P(),
    )
    return jax.shard_map(
        body,
        mesh=mesh,
        in_specs=placed,
        out_specs=(P("group", "blk", None), P("group", "blk", None), P("group", "blk", None)),
        check_vma=False,
    )
```

profile of v0, /device:TPU:19, one launch (start us, length us, event | category | flops | bytes accessed | tf_op | source)
XLA Modules:
  0.0 167.2 jit_solution(15250934654074469088)
XLA Ops:
  7.2 0.0 copy-start
  7.2 0.0 copy-start.1
  7.2 0.0 all-reduce.3.cloned.1.call-start
  7.2 1.3 dynamic_slice.8
  9.2 2.2 %select_bitcast_fusion = (bf16[512,512]{1,0:T(8,128)(2,1)}, bf16[512,512]{1,0:T(8,128)(2,1)}) fusion(bf16[1,512,512]{2,1,0:T(8,128)(2,1)} %param.8, pred[]{:T(512)S(6)} %eq.4, bf16[1,512,512]{2,1,0:T(8,128)(2,1)} %param.7), kind=kLoop, calls=%fused_computation.19 | loop fusion | flops 524288 | bytes 2097153 | tf_op jit(solution)/shard_map/jit(_where)/select_n | solution.py:14
  11.5 0.0 all-reduce.3.cloned.1.call-update
  11.5 0.0 all-gather.5.cloned.1.call-start
  11.6 78.5 %all-reduce.3.cloned.1.call-done = (bf16[512,512]{1,0:T(8,128)(2,1)}, bf16[512,512]{1,0:T(8,128)(2,1)}) async-done(((bf16[512,512]{1,0:T(8,128)(2,1)}, bf16[512,512]{1,0:T(8,128)(2,1)}), (bf16[512,512]{1,0:T(8,128)(2,1)}, bf16[512,512]{1,0:T(8,128)(2,1)})) %all-reduce.3.cloned.1.call-update) | async-done | bytes 1048592 | tf_op jit(solution)/shard_map/psum | solution.py:15
  90.0 0.0 all-gather.5.cloned.1.call-update
  90.0 0.0 all-gather.3.cloned.1.call-start
  90.1 0.7 all-gather.3.cloned.1.call-update
  90.8 0.0 copy-done.1
  90.8 0.4 reshape_squeeze.3
  91.2 0.2 multiply_cosine_fusion
  91.4 23.3 %all-gather.5.cloned.1.call-done = bf16[2048,512]{1,0:T(8,128)(2,1)} async-done(((bf16[512,512]{1,0:T(8,128)(2,1)}), bf16[2048,512]{1,0:T(8,128)(2,1)}) %all-gather.5.cloned.1.call-update) | async-done | bytes 2097168 | tf_op jit(solution)/shard_map/all_gather | solution.py:49
  114.7 0.0 copy-done
  114.7 2.3 %convolution_convert_fusion = bf16[512,128]{1,0:T(8,128)(2,1)S(1)} fusion(bf16[2048,512]{1,0:T(8,128)(2,1)} %all-gather.5.cloned.1.call-done, bf16[1,128,2048]{2,1,0:T(8,128)(2,1)S(1)} %copy-done), kind=kOutput, calls=%fused_computation.12 | convolution fusion | flops 268500992 | bytes 2752512 | tf_op jit(solution)/shard_map/dot_general | solution.py:52
  117.1 0.8 copy.17
  117.8 21.0 %all-gather.3.cloned.1.call-done = bf16[2048,512]{1,0:T(8,128)(2,1)} async-done(((bf16[512,512]{1,0:T(8,128)(2,1)}), bf16[2048,512]{1,0:T(8,128)(2,1)}) %all-gather.3.cloned.1.call-update) | async-done | bytes 2097168 | tf_op jit(solution)/shard_map/all_gather | solution.py:48
  138.9 2.3 %fusion.18 = f32[512,128]{1,0:T(8,128)S(1)} fusion(bf16[2048,512]{1,0:T(8,128)(2,1)} %all-gather.3.cloned.1.call-done, bf16[1,128,2048]{2,1,0:T(8,128)(2,1)S(1)} %copy-done), kind=kOutput, calls=%fused_computation.15 | convolution fusion | flops 268435456 | bytes 2883584 | tf_op jit(solution)/shard_map/dot_general | solution.py:51
  141.3 0.8 copy.22
  142.1 7.3 %all_gather.15 = bf16[512,512]{0,1:T(8,128)(2,1)S(1)} all-gather(bf16[128,512]{0,1:T(8,128)(2,1)S(1)} %bitcast.64), channel_id=1, replica_groups=mesh['blk'=4,'group'=8] {'blk'}, dimensions={0}, use_global_device_ids=true | all-gather | bytes 655360 | tf_op jit(solution)/shard_map/all_gather | solution.py:69
  149.4 7.3 %all_gather.14 = bf16[512,512]{0,1:T(8,128)(2,1)S(1)} all-gather(bf16[128,512]{0,1:T(8,128)(2,1)S(1)} %bitcast.62), channel_id=1, replica_groups=mesh['blk'=4,'group'=8] {'blk'}, dimensions={0}, use_global_device_ids=true | all-gather | bytes 655360 | tf_op jit(solution)/shard_map/all_gather | solution.py:68
  156.7 0.9 fusion.2
  157.6 0.9 fusion
  158.5 1.2 divide_convert_fusion
  159.6 1.0 copy.18
  (8 shorter events, 0.1 us)
Async XLA Ops:
  7.2 107.6 %copy-start = (bf16[1,128,2048]{2,1,0:T(8,128)(2,1)S(1)}, bf16[1,128,2048]{2,1,0:T(8,128)(2,1)}, u32[]{:S(2)}) copy-start(bf16[1,128,2048]{2,1,0:T(8,128)(2,1)} %param.6) | copy-start | bytes 1572868
  7.2 83.6 %copy-start.1 = (bf16[1,128,2048]{2,1,0:T(8,128)(2,1)S(1)}, bf16[1,128,2048]{2,1,0:T(8,128)(2,1)}, u32[]{:S(2)}) copy-start(bf16[1,128,2048]{2,1,0:T(8,128)(2,1)} %param.5) | copy-start | bytes 1572868
  7.2 82.8 %all-reduce.3.cloned.1.call-start = ((), (), s32[]{:S(2)}) async-start(), calls=%async_computation.2 | async-start | bytes 2097152 | tf_op jit(solution)/shard_map/psum | solution.py:15
  11.5 103.2 %all-gather.5.cloned.1.call-start = ((), (), s32[]{:S(2)}) async-start(), calls=%async_computation.1 | async-start | bytes 2621440 | tf_op jit(solution)/shard_map/all_gather | solution.py:49
  90.0 48.9 %all-gather.3.cloned.1.call-start = ((), (), s32[]{:S(2)}) async-start(), calls=%async_computation | async-start | bytes 2621440 | tf_op jit(solution)/shard_map/all_gather | solution.py:48
Sparse Core Ops, SparseCore 0:
  12.1 77.8 all-reduce.2
  91.6 23.1 all-gather.4
  116.3 22.5 all-gather.2
where the time goes:
time: 169 us; the launch traced here: 167 us
  waiting for transfers between devices  123 us (73%)
  blocking collectives  14.6 us (9%)
  between operations  14.5 us (9%)
  matrix products  6.71 us (4%)
  local copies, waits for them, and re-layouts  4.27 us (3%)
  other arithmetic  3.47 us (2%)
    psum x1, waiting for transfers between devices, spread(): return lax.psum(kept, axis)  78.5 us
    all_gather x1, waiting for transfers between devices, body(): lax.all_gather(shard_values, 'blk', axis=0, tiled=True)  23.3 us
    all_gather x1, waiting for transfers between devices, body(): lax.all_gather(shard_keys, 'blk', axis=0, tiled=True)  21 us
    all_gather x1, blocking collectives, body(): lax.all_gather(cache_values, 'blk', axis=0, tiled=True)  7.3 us
    all_gather x1, blocking collectives, body(): lax.all_gather(cache_keys, 'blk', axis=0, tiled=True)  7.29 us
  transfers between devices with their start and end apart: 3, of which 3 were waited for; matrix products, arithmetic and copies ran while one was open for 2% of the time, Pallas kernels for 0%

commit v1 on v0

v1 whole, which is shorter than its diff:
```python
import functools
import math

import jax
import jax.numpy as jnp
from jax import lax
from jax.experimental import pallas as pl
from jax.experimental.pallas import tpu as pltpu
from jax.sharding import PartitionSpec as P

QUERY_HEADS = 16
KEY_VALUE_HEADS = 4
HEAD_SIZE = 128
MESH = pl.DeviceIdType.MESH


def spread(value, axis, source):
    kept = jnp.where(lax.axis_index(axis) == source, value, 0).astype(value.dtype)
    return lax.psum(kept, axis)


def rotate(unshaped_rows, positions):
    half_dim = HEAD_SIZE // 2
    inverse_freq = jnp.exp(
        jnp.arange(half_dim).astype(jnp.float32) * (-2.0 * math.log(500000.0) / HEAD_SIZE)
    )
    angles = positions.astype(jnp.float32)[:, None] * inverse_freq[None, :]
    cos_table = jnp.cos(angles)[:, None, :]
    sin_table = jnp.sin(angles)[:, None, :]
    reshaped_rows = unshaped_rows.reshape(unshaped_rows.shape[0], KEY_VALUE_HEADS, HEAD_SIZE)
    first_half = reshaped_rows[..., :half_dim]
    second_half = reshaped_rows[..., half_dim:]
    transposed_rows = jnp.concatenate(
        [
            first_half * cos_table - second_half * sin_table,
            second_half * cos_table + first_half * sin_table,
        ],
        axis=-1,
    )
    return transposed_rows.reshape(unshaped_rows.shape[0], KEY_VALUE_HEADS * HEAD_SIZE)


def plain_body(queries, normed, key_weight_copies, value_weight_copies, owner):
    input_rows = normed[0]
    token_rows = input_rows.shape[0]
    owner_group = lax.dynamic_index_in_dim(owner, lax.axis_index("blk"), 0, keepdims=False)
    shards = (
        spread(key_weight_copies[0], "group", owner_group),
        spread(value_weight_copies[0], "group", owner_group),
    )
    pieces = [lax.all_gather(s, "blk", axis=0, tiled=True) for s in shards]
    key_raw = jnp.dot(input_rows, pieces[0], preferred_element_type=jnp.float32)
    value_raw = jnp.dot(input_rows, pieces[1], preferred_element_type=jnp.float32)
    positions = lax.axis_index("blk") * token_rows + jnp.arange(token_rows, dtype=jnp.int32)
    cache_keys = rotate(key_raw, positions).astype(jnp.bfloat16)
    cache_values = value_raw.astype(jnp.bfloat16)
    rep = QUERY_HEADS // KEY_VALUE_HEADS
    grid = queries[0].reshape(token_rows, KEY_VALUE_HEADS, rep, HEAD_SIZE)
    keys = lax.all_gather(cache_keys, "blk", axis=0, tiled=True)
    values = lax.all_gather(cache_values, "blk", axis=0, tiled=True)
    count = keys.shape[0]
    keys = keys.reshape(count, KEY_VALUE_HEADS, HEAD_SIZE)
    values = values.reshape(count, KEY_VALUE_HEADS, HEAD_SIZE)
    scores = jnp.einsum("lewc,jec->ewlj", grid, keys, preferred_element_type=jnp.float32)
    scores = scores * HEAD_SIZE ** (-0.5)
    allowed = jnp.arange(count, dtype=jnp.int32)[None, :] <= positions[:, None]
    scores = jnp.where(allowed, scores, -jnp.inf)
    probs = jnp.exp(scores - jnp.max(scores, axis=-1, keepdims=True))
    total = jnp.sum(probs, axis=-1)
    weighted = jnp.einsum(
        "lxbp,plj->lxbj", probs.astype(jnp.bfloat16), values, preferred_element_type=jnp.float32
    )
    attended = (weighted / total[..., None]).transpose(2, 0, 1, 3)
    attended = attended.reshape(token_rows, QUERY_HEADS * HEAD_SIZE).astype(jnp.bfloat16)
    return (cache_keys[None], cache_values[None], attended[None])


def kernel(
    dims, owner_ref, q_hbm, n_hbm, wk_hbm, wv_hbm, ck_ref, cv_ref, at_ref,
    qbuf, nbuf, ybuf, merged, zbuf, other, wb, proj, cos_t, sin_t, kvbuf, top, tot, acc,
    loc_sem, own_sem, y_send, y_recv, z_send, z_recv, n_send, n_recv, c_send, c_recv,
    gz_send, gy_send, gx_send, g_recv, p_send, p_recv, k_send, k_recv, f_send, f_recv,
):
    X, Z, Y = dims
    G = Z * Y
    T = q_hbm.shape[1]
    ch = wb.shape[2]
    half = HEAD_SIZE // 2
    g, b = lax.axis_index("group"), lax.axis_index("blk")
    z, y = g // Y, g % Y
    x, core = b // 2, b % 2
    twin = x * 2 + 1 - core

    def at(group, blk):
        return {"group": group, "blk": blk}

    def remote(src, dst, ss, rs, dev):
        return pltpu.make_async_remote_copy(
            src_ref=src, dst_ref=dst, send_sem=ss, recv_sem=rs, device_id=dev, device_id_type=MESH
        )

    z_others = [lax.rem(z + i, Z) for i in range(1, Z)]
    y_others = [lax.rem(y + i, Y) for i in range(1, Y)]
    x_others = [lax.rem(x + i, X) for i in range(1, X)]
    barrier = pltpu.get_barrier_semaphore()
    peers = [at(z * Y + yp, b) for yp in y_others]
    peers += [at(zp * Y + y, b) for zp in z_others]
    peers += [at(g, xp * 2 + core) for xp in x_others]
    peers += [at(g, twin)]
    for dev in peers:
        pl.semaphore_signal(barrier, inc=1, device_id=dev, device_id_type=MESH)

    z_order = z_others + [z]
    weights = (wk_hbm, wv_hbm)
    own = []
    for i, zp in enumerate(z_order):
        for k in range(2):
            rows = pl.ds(pl.multiple_of((zp * Y + y) * ch, ch), ch)
            cp = pltpu.make_async_copy(
                weights[k].at[0, rows], ybuf.at[y, zp, k], own_sem.at[i, k]
            )
            cp.start()
            own.append(cp)
    q_copy = pltpu.make_async_copy(q_hbm.at[0], qbuf, loc_sem.at[0])
    n_copy = pltpu.make_async_copy(n_hbm.at[0], nbuf.at[core], loc_sem.at[1])
    n_copy.start()
    q_copy.start()

    pl.semaphore_wait(barrier, len(peers))

    sends = []
    for zp in z_order:
        for yp in y_others:
            for k in range(2):
                rows = pl.ds(pl.multiple_of((zp * Y + yp) * ch, ch), ch)
                cp = remote(
                    weights[k].at[0, rows], ybuf.at[y, zp, k],
                    y_send.at[yp, zp, k], y_recv.at[y, zp, k], at(z * Y + yp, b),
                )
                cp.start()
                sends.append(cp)
    n_send_copy = remote(n_hbm.at[0], nbuf.at[core], n_send, n_recv, at(g, twin))
    n_send_copy.start()

    pos = (x * 2 * T + lax.broadcasted_iota(jnp.int32, (2 * T, HEAD_SIZE), 0)).astype(jnp.float32)
    lane = lax.broadcasted_iota(jnp.int32, (2 * T, HEAD_SIZE), 1)
    freq = jnp.exp((lane % half).astype(jnp.float32) * (-2.0 * math.log(500000.0) / HEAD_SIZE))
    angle = pos * freq
    cos_t[...] = jnp.cos(angle)
    sin_a = jnp.sin(angle)
    sin_t[...] = jnp.where(lane < half, -sin_a, sin_a)

    owner_group = owner_ref[b]
    owner_z, owner_y = owner_group // Y, owner_group % Y

    def pick(which, options):
        sel = options[0]
        for i in range(1, len(options)):
            sel = lax.select(which == i, options[i], sel)
        return sel

    for i, zp in enumerate(z_order):
        for k in range(2):
            own[2 * i + k].wait()
            for yp in y_others:
                pltpu.make_async_copy(
                    ybuf.at[yp, zp, k], ybuf.at[yp, zp, k], y_recv.at[yp, zp, k]
                ).wait()
        for k in range(2):
            sel = pick(owner_y, [ybuf[yy, zp, k] for yy in range(Y)])
            if i < Z - 1:
                merged[i, k] = sel
            else:
                zbuf[z, k] = sel
        if i < Z - 1:
            cp = remote(merged.at[i], zbuf.at[z], z_send.at[i], z_recv.at[z], at(zp * Y + y, b))
            cp.start()
            sends.append(cp)
    for zp in reversed(z_others):
        pltpu.make_async_copy(zbuf.at[zp], zbuf.at[zp], z_recv.at[zp]).wait()

    other[...] = pick(owner_z, [zbuf[zz, 1 - core] for zz in range(Z)])
    cp = remote(other, wb.at[b, g], c_send, c_recv, at(g, twin))
    cp.start()
    sends.append(cp)
    wb[b, g] = pick(owner_z, [zbuf[zz, core] for zz in range(Z)])
    pltpu.make_async_copy(wb.at[twin, g], wb.at[twin, g], c_recv).wait()

    def piece(xx, gg):
        return wb.at[pl.ds(2 * xx, 2), gg]

    def give(gg, ss, group, xx):
        cp = remote(piece(x, gg), piece(x, gg), ss, g_recv.at[x, gg], at(group, xx * 2 + core))
        cp.start()
        sends.append(cp)

    def arrived(xx, gg):
        pltpu.make_async_copy(piece(xx, gg), piece(xx, gg), g_recv.at[xx, gg]).wait()

    def to_x(gg):
        for xp in x_others:
            give(gg, gx_send.at[xp, gg], g, xp)

    def to_y(gg, zz):
        for yp in y_others:
            give(gg, gy_send.at[yp, zz], z * Y + yp, x)

    to_x(g)
    for zp in z_others:
        give(g, gz_send.at[zp], zp * Y + y, x)
    to_y(g, z)
    for zp in reversed(z_others):
        arrived(x, zp * Y + y)
        to_y(zp * Y + y, zp)
        to_x(zp * Y + y)
    for zp in [z] + z_others[::-1]:
        for yp in y_others:
            arrived(x, zp * Y + yp)
            to_x(zp * Y + yp)

    n_copy.wait()
    pltpu.make_async_copy(nbuf.at[1 - core], nbuf.at[1 - core], n_recv).wait()
    depth = 2 * G * ch
    cols = wb.shape[3]

    def product(xx):
        feats = pl.ds(pl.multiple_of(xx * depth, depth), depth)
        left = nbuf[:, :, feats].reshape(2 * T, depth)
        right = wb[pl.ds(2 * xx, 2)].reshape(depth, cols)
        return jnp.dot(left, right, preferred_element_type=jnp.float32)

    proj[...] = product(x)
    for xp in x_others:
        for zp in [z] + z_others[::-1]:
            arrived(xp, zp * Y + y)
        for zp in [z] + z_others[::-1]:
            for yp in y_others:
                arrived(xp, zp * Y + yp)
        proj[...] += product(xp)

    heads = [slice(h * HEAD_SIZE, (h + 1) * HEAD_SIZE) for h in range(KEY_VALUE_HEADS)]

    @pl.when(core == 0)
    def _():
        for hs in heads:
            part = proj[:, hs]
            turned = part * cos_t[...] + pltpu.roll(part, half, 1) * sin_t[...]
            kvbuf[0, x, :, hs] = turned.astype(jnp.bfloat16)

    @pl.when(core == 1)
    def _():
        kvbuf[1, x] = proj[...].astype(jnp.bfloat16)

    mine = kvbuf.at[core, x]
    for xp in range(X):
        @pl.when(xp > x)
        def _():
            remote(mine, mine, k_send.at[xp], k_recv.at[x], at(g, xp * 2 + core)).start()
    twin_copy = remote(mine, mine, p_send, p_recv, at(g, twin))
    twin_copy.start()
    q_copy.wait()
    theirs = kvbuf.at[1 - core, x]
    pltpu.make_async_copy(theirs, theirs, p_recv).wait()

    span = pl.ds(pl.multiple_of(core * T, T), T)
    ck_ref[0] = kvbuf[0, x, span, :]
    cv_ref[0] = kvbuf[1, x, span, :]

    rep = QUERY_HEADS // KEY_VALUE_HEADS
    scale = HEAD_SIZE ** (-0.5) * math.log2(math.e)

    def scored(h, xx):
        stacked = jnp.concatenate(
            [
                qbuf[:, (h * rep + j) * HEAD_SIZE : (h * rep + j + 1) * HEAD_SIZE]
                for j in range(rep)
            ],
            axis=0,
        )
        return lax.dot_general(
            stacked, kvbuf[0, xx, :, heads[h]], (((1,), (1,)), ((), ())),
            preferred_element_type=jnp.float32,
        )

    for h in range(KEY_VALUE_HEADS):
        s = scored(h, x)
        row = core * T + lax.rem(lax.broadcasted_iota(jnp.int32, s.shape, 0), T)
        s = jnp.where(lax.broadcasted_iota(jnp.int32, s.shape, 1) <= row, s, -jnp.inf)
        m = jnp.max(s, axis=1, keepdims=True)
        p = jnp.exp2((s - m) * scale)
        top[h] = m
        tot[h] = jnp.sum(p, axis=1, keepdims=True)
        acc[h] = jnp.dot(
            p.astype(jnp.bfloat16), kvbuf[1, x, :, heads[h]], preferred_element_type=jnp.float32
        )

    for xs in range(X):
        @pl.when(xs < x)
        def _():
            got = kvbuf.at[core, xs]
            pltpu.make_async_copy(got, got, k_recv.at[xs]).wait()
            remote(got, got, f_send.at[xs], f_recv.at[xs], at(g, twin)).start()
            rest = kvbuf.at[1 - core, xs]
            pltpu.make_async_copy(rest, rest, f_recv.at[xs]).wait()
            for h in range(KEY_VALUE_HEADS):
                s = scored(h, xs)
                old = top[h]
                m = jnp.maximum(old, jnp.max(s, axis=1, keepdims=True))
                fade = jnp.exp2((old - m) * scale)
                p = jnp.exp2((s - m) * scale)
                top[h] = m
                tot[h] = tot[h] * fade + jnp.sum(p, axis=1, keepdims=True)
                acc[h] = acc[h] * fade + jnp.dot(
                    p.astype(jnp.bfloat16), kvbuf[1, xs, :, heads[h]],
                    preferred_element_type=jnp.float32,
                )

    for h in range(KEY_VALUE_HEADS):
        done = (acc[h] / tot[h]).astype(jnp.bfloat16)
        for j in range(rep):
            at_ref[0, :, (h * rep + j) * HEAD_SIZE : (h * rep + j + 1) * HEAD_SIZE] = done[
                j * T : (j + 1) * T
            ]

    for cp in sends:
        cp.wait_send()
    n_send_copy.wait_send()
    twin_copy.wait_send()
    for xp in range(X):
        @pl.when(xp > x)
        def _():
            remote(mine, mine, k_send.at[xp], k_recv.at[x], at(g, xp * 2 + core)).wait_send()

        @pl.when(xp < x)
        def _():
            got = kvbuf.at[core, xp]
            remote(got, got, f_send.at[xp], f_recv.at[xp], at(g, twin)).wait_send()


def fused_body(dims, queries, normed, key_weight_copies, value_weight_copies, owner):
    X, Z, Y = dims
    G = Z * Y
    _, T, qcols = queries.shape
    feats = normed.shape[2]
    _, shard_rows, cols = key_weight_copies.shape
    ch = shard_rows // G
    bf, f32 = jnp.bfloat16, jnp.float32
    rep = QUERY_HEADS // KEY_VALUE_HEADS
    vm, dma = pltpu.VMEM, pltpu.SemaphoreType.DMA
    anyspace = pl.BlockSpec(memory_space=pl.ANY)
    vmem = pl.BlockSpec(memory_space=pltpu.VMEM)
    return pl.pallas_call(
        functools.partial(kernel, dims),
        out_shape=(
            jax.ShapeDtypeStruct((1, T, cols), bf),
            jax.ShapeDtypeStruct((1, T, cols), bf),
            jax.ShapeDtypeStruct((1, T, qcols), bf),
        ),
        in_specs=[pl.BlockSpec(memory_space=pltpu.SMEM)] + [anyspace] * 4,
        out_specs=(vmem, vmem, vmem),
        scratch_shapes=[
            vm((T, qcols), bf),
            vm((2, T, feats), bf),
            vm((Y, Z, 2, ch, cols), bf),
            vm((max(Z - 1, 1), 2, ch, cols), bf),
            vm((Z, 2, ch, cols), bf),
            vm((ch, cols), bf),
            vm((2 * X, G, ch, cols), bf),
            vm((2 * T, cols), f32),
            vm((2 * T, HEAD_SIZE), f32),
            vm((2 * T, HEAD_SIZE), f32),
            vm((2, X, 2 * T, cols), bf),
            vm((KEY_VALUE_HEADS, rep * T, 1), f32),
            vm((KEY_VALUE_HEADS, rep * T, 1), f32),
            vm((KEY_VALUE_HEADS, rep * T, HEAD_SIZE), f32),
            dma((2,)),
            dma((Z, 2)),
            dma((Y, Z, 2)),
            dma((Y, Z, 2)),
            dma((Z,)),
            dma((Z,)),
            dma,
            dma,
            dma,
            dma,
            dma((Z,)),
            dma((Y, Z)),
            dma((X, G)),
            dma((X, G)),
            dma,
            dma,
            dma((X,)),
            dma((X,)),
            dma((X,)),
            dma((X,)),
        ],
        compiler_params=pltpu.CompilerParams(
            collective_id=0, has_side_effects=True, vmem_limit_bytes=48 * 1024 * 1024
        ),
    )(owner, queries, normed, key_weight_copies, value_weight_copies)


def body(sizes, *args):
    n_blk, n_group = sizes
    shard_rows = args[2].shape[1]
    minor = 1
    while 2 * (2 * minor) ** 2 <= n_group:
        minor *= 2
    aligned = n_group % minor == 0 and shard_rows % (16 * n_group) == 0 and n_blk % 2 == 0
    if not aligned or args[0].shape[1] % 128:
        return plain_body(*args)
    return fused_body((n_blk // 2, n_group // minor, minor), *args)


def solution(mesh):
    split = P("group", "blk", None)
    return jax.shard_map(
        functools.partial(body, (mesh.shape["blk"], mesh.shape["group"])),
        mesh=mesh,
        in_specs=(split, split, split, split, P()),
        out_specs=(split, split, split),
        check_vma=False,
    )
```

time: 169 us -> 74.6 us (0.44)
  waiting for transfers between devices: 123 us -> 0 us
  Pallas kernels: 0 us -> 66.7 us
  blocking collectives: 14.6 us -> 0 us
  between operations: 14.5 us -> 0.65 us
  matrix products: 6.71 us -> 0 us
  other arithmetic: 3.47 us -> 0 us
  local copies, waits for them, and re-layouts: 4.27 us -> 6.92 us
    psum x1 -> x0, waiting for transfers between devices: 78.5 us -> none  [spread(): return lax.psum(kept, axis)]
    pallas_call x0 -> x1, Pallas kernels: none -> 66.7 us  [fused_body(): pl.pallas_call(functools.partial(kernel, dims), out_shape=(jax.ShapeDtype...]
    all_gather x2 -> x0, waiting for transfers between devices: 44.3 us -> none  [the longest x1 23.3 us: body(): lax.all_gather(shard_values, 'blk', axis=0, tiled=True)]
    all_gather x2 -> x0, blocking collectives: 14.6 us -> none  [the longest x1 7.3 us: body(): lax.all_gather(cache_values, 'blk', axis=0, tiled=True)]
    dot_general x4 -> x0, matrix products: 6.71 us -> none  [the longest x1 2.34 us: body(): jnp.dot(input_rows, pieces[1], preferred_element_type=jnp.float32)]
    unnamed x6 -> x13, local copies, waits for them, and re-layouts: 1.79 us -> 6.92 us
    select_n x1 -> x0, other arithmetic: 2.25 us -> none  [spread(): jnp.where(lax.axis_index(axis) == source, value, 0).astype(value.dtype)]
  transfers between devices with their start and end apart: 3 -> 0, of which waited for: 3 -> 0; matrix products, arithmetic and copies ran while one was open for 2% -> 0% of each run, Pallas kernels for 0% -> 0%
where the time goes in v1:
time: 74.6 us; the launch traced here: 74.3 us
  Pallas kernels  66.7 us (89%)
  local copies, waits for them, and re-layouts  6.92 us (9%)
    pallas_call x1, Pallas kernels, fused_body(): pl.pallas_call(functools.partial(kernel, dims), out_shape=(jax.ShapeDtype...  66.7 us
    unnamed x13, local copies, waits for them, and re-layouts  6.92 us

profile of v1, /device:TPU:19, one launch (start us, length us, event | category | flops | bytes accessed | tf_op | source)
XLA Modules:
  0.0 74.3 jit_solution(6511538363893286566)
XLA Ops:
  0.6 0.0 copy-start
  0.6 1.0 %copy-done = bf16[1,128,2048]{2,1,0:T(8,128)(2,1)S(1)} copy-done((bf16[1,128,2048]{2,1,0:T(8,128)(2,1)S(1)}, bf16[1,128,2048]{2,1,0:T(8,128)(2,1)}, u32[]{:S(2)}) %copy-start) | copy-done | bytes 524312
  1.7 0.0 copy-start.1
  1.7 1.0 %copy-done.1 = bf16[1,128,2048]{2,1,0:T(8,128)(2,1)S(1)} copy-done((bf16[1,128,2048]{2,1,0:T(8,128)(2,1)S(1)}, bf16[1,128,2048]{2,1,0:T(8,128)(2,1)}, u32[]{:S(2)}) %copy-start.1) | copy-done | bytes 524312
  2.7 0.0 copy-start.2
  2.7 1.0 %copy-done.2 = bf16[1,512,512]{2,1,0:T(8,128)(2,1)S(1)} copy-done((bf16[1,512,512]{2,1,0:T(8,128)(2,1)S(1)}, bf16[1,512,512]{2,1,0:T(8,128)(2,1)}, u32[]{:S(2)}) %copy-start.2) | copy-done | bytes 524312
  3.8 0.0 copy-start.3
  3.8 1.0 %copy-done.3 = bf16[1,512,512]{2,1,0:T(8,128)(2,1)S(1)} copy-done((bf16[1,512,512]{2,1,0:T(8,128)(2,1)S(1)}, bf16[1,512,512]{2,1,0:T(8,128)(2,1)}, u32[]{:S(2)}) %copy-start.3) | copy-done | bytes 524312
  4.8 0.0 copy-start.4
  4.8 0.7 copy-done.4
  5.5 66.7 %shard_map.76 = (bf16[1,128,512]{2,1,0:T(8,128)(2,1)S(1)}, bf16[1,128,512]{2,1,0:T(8,128)(2,1)S(1)}, bf16[1,128,2048]{2,1,0:T(8,128)(2,1)S(1)}) custom-call(s32[4]{0:T(128)S(1)} %copy-done.4, bf16[1,128,2048]{2,1,0:T(8,128)(2,1)S(1)} %copy-done, bf16[1,128,2048]{2,1,0:T(8,128)(2,1)S(1)} %copy-done.1, bf16[1,512,512]{2,1,0:T(8,128)(2,1)S(1)} %copy-done.2, ...), custom_call_target="tpu_custom_call" | custom-call | tf_op jit(solution)/shard_map/pallas_call | solution.py:352
  72.2 0.7 copy.11
  72.8 0.7 copy.12
  73.5 0.8 %copy.13 = bf16[1,128,2048]{2,1,0:T(8,128)(2,1)} copy(bf16[1,128,2048]{2,1,0:T(8,128)(2,1)S(1)} %get-tuple-element.8) | data formatting | bytes 1048576
Async XLA Ops:
  0.6 1.0 %copy-start = (bf16[1,128,2048]{2,1,0:T(8,128)(2,1)S(1)}, bf16[1,128,2048]{2,1,0:T(8,128)(2,1)}, u32[]{:S(2)}) copy-start(bf16[1,128,2048]{2,1,0:T(8,128)(2,1)} %q_hbm.1) | copy-start | bytes 1572868
  1.7 1.0 %copy-start.1 = (bf16[1,128,2048]{2,1,0:T(8,128)(2,1)S(1)}, bf16[1,128,2048]{2,1,0:T(8,128)(2,1)}, u32[]{:S(2)}) copy-start(bf16[1,128,2048]{2,1,0:T(8,128)(2,1)} %n_hbm.1) | copy-start | bytes 1572868
  2.7 1.0 %copy-start.2 = (bf16[1,512,512]{2,1,0:T(8,128)(2,1)S(1)}, bf16[1,512,512]{2,1,0:T(8,128)(2,1)}, u32[]{:S(2)}) copy-start(bf16[1,512,512]{2,1,0:T(8,128)(2,1)} %wk_hbm.1) | copy-start | bytes 1572868
  3.8 1.0 %copy-start.3 = (bf16[1,512,512]{2,1,0:T(8,128)(2,1)S(1)}, bf16[1,512,512]{2,1,0:T(8,128)(2,1)}, u32[]{:S(2)}) copy-start(bf16[1,512,512]{2,1,0:T(8,128)(2,1)} %wv_hbm.1) | copy-start | bytes 1572868
  4.8 0.7 copy-start.4
